TPU v7x, 256 devices: a whole 4x4x8 slice. The times are simulated.
256 devices in a mesh: row: 8 (over y, core), col: 32 (over x, z).
Axes of the slice: x: 4, y: 4, z: 8, core: 2. Of those that a mesh axis runs over, the one named last changes fastest.
Arguments:
- inner_base: bfloat16 [4, 1, 2, 4096, 14336], P(None, None, None, 'row', 'col'), may hold values from -250 to 250
- inner_left: bfloat16 [4, 1, 2, 4096, 16], P(None, None, None, ('row', 'col')), may hold values from -6 to 6
- inner_right: bfloat16 [4, 1, 2, 16, 14336], P(None, None, None, 'row', 'col'), may hold values from -12 to 12
- inner_mag: float32 [4, 1, 2, 14336], P(None, None, None, 'col'), may hold values from 512 to 2048
- outer_base: bfloat16 [4, 1, 14336, 4096], P(None, None, 'row', 'col'), may hold values from -250 to 250
- outer_left: bfloat16 [4, 1, 14336, 16], P(None, None, ('row', 'col')), may hold values from -6 to 6
- outer_right: bfloat16 [4, 1, 16, 4096], P(None, None, 'row', 'col'), may hold values from -12 to 12
- outer_mag: float32 [4, 1, 4096], P(None, None, 'col'), may hold values from 1792 to 7168
Outputs:
- inner_merged: bfloat16 [4, 1, 2, 4096, 14336], P(None, None, None, 'row', 'col')
- outer_merged: bfloat16 [4, 1, 14336, 4096], P(None, None, 'row', 'col')
All inputs are finite; a program needn't handle non-finite values.
Results may differ from a plain program's by a relative error of at most 0.001.
Values may be sent and summed in bfloat16 or wider, within the bound.
No kernel may reach another device: no remote copies, remote signals or barrier semaphores. Data moves between devices by JAX's collectives and lax.ppermute only.
A program may use at most 64 MiB of HBM per device.

v0:
```python
import jax
import jax.numpy as jnp
from jax import lax
from jax.sharding import PartitionSpec as P

epsilon = 1e-06


def from_everyone(value, axis):
    size = lax.axis_size(axis)
    return lax.all_to_all(
        jnp.broadcast_to(value[None], (size, *value.shape)), axis, 0, 0, tiled=True
    )


def over_copies(value, axis):
    return from_everyone(value, axis).sum(axis=0)


def packed_total(arrays, axis):
    line, at, finished = (jnp.concatenate([a.reshape(-1) for a in arrays]), 0, [])
    subtotal = over_copies(line, axis)
    for a in arrays:
        finished.append(subtotal[at : at + a.size].reshape(a.shape))
        at += a.size
    return tuple(finished)


def in_order(tiles, dim):
    lengths = list(tiles.shape[1:])
    lengths[dim] *= tiles.shape[0]
    return jnp.moveaxis(tiles, 0, dim).reshape(lengths)


def gathered_copies(value, axis, dim):
    tiles = from_everyone(value, axis)
    return in_order(tiles, dim)


def turned_gather(arrays, axis, dims):
    turned = [jnp.moveaxis(a, dim, 0) for a, dim in zip(arrays, dims)]
    both = jnp.concatenate([t.reshape(len(t), -1) for t in turned], axis=1)
    result, at, finished = (lax.all_gather(both, axis, axis=0, tiled=True), 0, [])
    for t, dim in zip(turned, dims):
        section = result[:, at : at + t[0].size].reshape(-1, *t.shape[1:])
        finished.append(jnp.moveaxis(section, 0, dim))
        at += t[0].size
    return tuple(finished)


def combine_tile(base, left, right):
    delta = jnp.einsum("...ik,...kj->...ij", left, right, preferred_element_type=jnp.float32)
    return base.astype(jnp.float32) + delta


def merge_layer(
    inner_base, outer_base, inner_mag, outer_mag, inner_left, outer_left, inner_right, outer_right
):
    inner_full = combine_tile(inner_base, inner_left, inner_right)
    outer_full = combine_tile(outer_base, outer_left, outer_right)
    inner_squares = jnp.sum(inner_full * inner_full, axis=-2)
    outer_squares = jnp.sum(outer_full * outer_full, axis=-2)
    inner_totals, outer_totals = packed_total((inner_squares, outer_squares), "row")
    inner_scale = lax.rsqrt(inner_totals + epsilon)
    outer_scale = lax.rsqrt(outer_totals + epsilon)
    inner_factor = inner_mag * inner_scale
    outer_factor = outer_mag * outer_scale
    inner_merged = (inner_factor[..., None, :] * inner_full).astype(jnp.bfloat16)
    outer_merged = (outer_factor[..., None, :] * outer_full).astype(jnp.bfloat16)
    return (inner_merged, outer_merged)


def shards(
    inner_base, inner_left, inner_right, inner_mag, outer_base, outer_left, outer_right, outer_mag
):
    layer_count = inner_base.shape[0]
    inner_outputs = []
    outer_outputs = []
    inner_rows, outer_rows = (
        gathered_copies(inner_left, "col", 3),
        gathered_copies(outer_left, "col", 2),
    )
    inner_ranks, outer_ranks = turned_gather((inner_right, outer_right), "row", (3, 2))
    for layer_index in range(layer_count):
        inner_merged, outer_merged = merge_layer(
            inner_base[layer_index],
            outer_base[layer_index],
            inner_mag[layer_index],
            outer_mag[layer_index],
            inner_rows[layer_index],
            outer_rows[layer_index],
            inner_ranks[layer_index],
            outer_ranks[layer_index],
        )
        inner_outputs.append(inner_merged)
        outer_outputs.append(outer_merged)
    return (jnp.stack(inner_outputs), jnp.stack(outer_outputs))


def solution(mesh):
    in_specs = (
        P(None, None, None, "row", "col"),
        P(None, None, None, ("row", "col"), None),
        P(None, None, None, "row", "col"),
        P(None, None, None, "col"),
        P(None, None, "row", "col"),
        P(None, None, ("row", "col"), None),
        P(None, None, "row", "col"),
        P(None, None, "col"),
    )
    out_specs = (P(None, None, None, "row", "col"), P(None, None, "row", "col"))
    return jax.shard_map(shards, mesh=mesh, in_specs=in_specs, out_specs=out_specs, check_vma=False)
```

profile of v0, /device:TPU:1, one launch (start us, length us, event | category | flops | bytes accessed | tf_op | source)
XLA Modules:
  0.0 110.4 jit_solution(7065436759786785537)
XLA Ops:
  0.7 0.9 copy.81
  1.5 0.2 broadcast_bitcast_fusion
  1.7 1.8 %reshape.406 = bf16[32,2,1024]{2,1,0:T(2,128)(2,1)} reshape(bf16[32,4,1,2,16,16]{5,4,3,2,1,0:T(8,128)(2,1)S(1)} %broadcast_bitcast_fusion) | data formatting | bytes 262144
  3.5 11.9 %all-to-all-start = ((bf16[32,2,1024]{2,1,0:T(2,128)(2,1)}), bf16[32,2,1024]{2,1,0:T(2,128)(2,1)S(1)}, u32[]{:S(2)}, u32[]{:S(2)}) async-start(bf16[32,2,1024]{2,1,0:T(2,128)(2,1)} %reshape.406), calls=%async_computation | async-start | bytes 262144 | tf_op jit(solution)/shard_map/all_to_all | solution.py:11
  15.7 1.6 %fusion.20 = (bf16[1,1,1792,128]{3,2,1,0:T(8,128)(2,1)S(1)}, bf16[1,1,1792,128]{3,2,1,0:T(8,128)(2,1)S(1)}, bf16[1,1,1792,128]{3,2,1,0:T(8,128)(2,1)S(1)}, bf16[1,1,1792,128]{3,2,1,0:T(8,128)(2,1)S(1)}) fusion(bf16[4,1,1792,128]{3,2,1,0:T(8,128)(2,1)} %param.12), kind=kLoop, calls=%fused_computation.68 | loop fusion | bytes 3670016 | tf_op jit(solution)/shard_map/slice | solution.py:87
  17.3 14.1 %all-gather = bf16[8,2,4096]{2,1,0:T(2,128)(2,1)S(1)} all-gather(bf16[1,2,4096]{2,1,0:T(2,128)(2,1)S(1)} %maximum_bitcast_fusion), channel_id=1, replica_groups=mesh['row'=8,'col'=32] {'row'}, dimensions={0}, use_global_device_ids=true | all-gather | bytes 147456 | tf_op jit(solution)/shard_map/all_gather | solution.py:43
  31.7 1.7 %reshape.408 = bf16[32,2,1792]{2,1,0:T(2,128)(2,1)} reshape(bf16[32,4,1,16,56]{4,3,2,1,0:T(8,128)(2,1)S(1)} %broadcast_bitcast_fusion.1) | data formatting | bytes 458752
  33.3 1.0 copy.107
  34.3 1.0 copy.109
  35.3 1.0 copy.108
  36.3 0.2 copy.110
  36.6 9.5 %all-to-all-start.1 = ((bf16[32,2,1792]{2,1,0:T(2,128)(2,1)}), bf16[32,2,1792]{2,1,0:T(2,128)(2,1)S(1)}, u32[]{:S(2)}, u32[]{:S(2)}) async-start(bf16[32,2,1792]{2,1,0:T(2,128)(2,1)} %reshape.408), calls=%async_computation.1 | async-start | bytes 458752 | tf_op jit(solution)/shard_map/all_to_all | solution.py:11
  46.1 0.7 reshape.407
  46.8 0.2 bitcast_bitcast_fusion
  47.3 0.3 reshape.376
  47.7 0.3 reshape.392
  48.1 0.3 reshape.387
  48.5 0.3 reshape.382
  48.8 2.9 %multiply_reduce_fusion.2 = (f32[2,448]{1,0:T(2,128)S(1)}, f32[2,512,448]{1,2,0:T(8,128)}) fusion(bf16[2,512,16]{1,2,0:T(8,128)(2,1)S(1)} %reshape.382, bf16[4,1,2,16,448]{4,3,2,1,0:T(8,128)(2,1)S(1)} %bitcast.187, bf16[4,1,2,512,448]{3,4,2,1,0:T(8,128)(2,1)} %param.8), kind=kOutput, calls=%fused_computation.19 | convolution fusion | flops 16514176 | bytes 2821632 | tf_op jit(solution)/shard_map/...ik,...kj->...ij/dot_general | solution.py:52
  51.8 2.9 %multiply_reduce_fusion.1 = (f32[2,448]{1,0:T(2,128)S(1)}, f32[2,512,448]{1,2,0:T(8,128)}) fusion(bf16[2,512,16]{1,2,0:T(8,128)(2,1)S(1)} %reshape.387, bf16[4,1,2,16,448]{4,3,2,1,0:T(8,128)(2,1)S(1)} %bitcast.188, bf16[4,1,2,512,448]{3,4,2,1,0:T(8,128)(2,1)} %param.8), kind=kOutput, calls=%fused_computation.17 | convolution fusion | flops 16514176 | bytes 2821632 | tf_op jit(solution)/shard_map/...ik,...kj->...ij/dot_general | solution.py:52
  54.8 2.9 %multiply_reduce_fusion = (f32[2,448]{1,0:T(2,128)S(1)}, f32[2,512,448]{1,2,0:T(8,128)}) fusion(bf16[2,512,16]{1,2,0:T(8,128)(2,1)S(1)} %reshape.392, bf16[4,1,2,16,448]{4,3,2,1,0:T(8,128)(2,1)S(1)} %bitcast.189, bf16[4,1,2,512,448]{3,4,2,1,0:T(8,128)(2,1)} %param.8), kind=kOutput, calls=%fused_computation.15 | convolution fusion | flops 16514176 | bytes 2821632 | tf_op jit(solution)/shard_map/...ik,...kj->...ij/dot_general | solution.py:52
  57.7 2.9 %multiply_reduce_fusion.3 = (f32[2,448]{1,0:T(2,128)S(1)}, f32[2,512,448]{1,2,0:T(8,128)}) fusion(bf16[2,512,16]{1,2,0:T(8,128)(2,1)S(1)} %reshape.376, bf16[4,1,2,16,448]{4,3,2,1,0:T(8,128)(2,1)S(1)} %bitcast.190, bf16[4,1,2,512,448]{3,4,2,1,0:T(8,128)(2,1)} %param.8), kind=kOutput, calls=%fused_computation.21 | convolution fusion | flops 16514176 | bytes 2821632 | tf_op jit(solution)/shard_map/...ik,...kj->...ij/dot_general | solution.py:52
  60.7 0.9 reshape.409
  62.0 0.2 reshape.395
  62.2 0.2 reshape.390
  62.7 0.4 multiply_reduce_fusion.7
  63.1 0.6 broadcast_in_dim.20
  63.7 4.2 %all-to-all-start.2 = ((f32[8,1,1024]{2,1,0:T(1,128)}), f32[8,1,1024]{2,1,0:T(1,128)S(1)}, u32[]{:S(2)}, u32[]{:S(2)}) async-start(f32[8,1,1024]{2,1,0:T(1,128)} %broadcast_in_dim.20), calls=%async_computation.2 | async-start | bytes 65536 | tf_op jit(solution)/shard_map/all_to_all | solution.py:11
  67.9 0.4 multiply_reduce_fusion.5
  68.3 1.4 %multiply_reduce_fusion.6 = (f32[128]{0:T(128)S(1)}, f32[1792,128]{0,1:T(8,128)S(1)}) fusion(bf16[1792,16]{0,1:T(8,128)(2,1)S(1)} %reshape.385, bf16[1,1,16,128]{3,0,2,1:T(2,128)(2,1)S(1)} %get-tuple-element.35, bf16[1,1,1792,128]{2,3,1,0:T(8,128)(2,1)} %copy.108), kind=kOutput, calls=%fused_computation.32 | convolution fusion | flops 8257408 | bytes 1438208 | tf_op jit(solution)/shard_map/...ik,...kj->...ij/dot_general | solution.py:52
  69.7 1.2 %multiply_reduce_fusion.4 = (f32[128]{0:T(128)S(1)}, f32[1792,128]{0,1:T(8,128)}) fusion(bf16[1792,16]{0,1:T(8,128)(2,1)S(1)} %reshape.395, bf16[1,1,16,128]{3,0,2,1:T(2,128)(2,1)S(1)} %get-tuple-element.33, bf16[1,1,1792,128]{2,3,1,0:T(8,128)(2,1)S(1)} %copy.110), kind=kOutput, calls=%fused_computation.30 | convolution fusion | flops 8257408 | bytes 1438208 | tf_op jit(solution)/shard_map/...ik,...kj->...ij/dot_general | solution.py:52
  71.0 1.6 %all-to-all-done.2 = f32[8,1,1024]{2,1,0:T(1,128)S(1)} async-done(((f32[8,1,1024]{2,1,0:T(1,128)}), f32[8,1,1024]{2,1,0:T(1,128)S(1)}, u32[]{:S(2)}, u32[]{:S(2)}) %all-to-all-start.2) | async-done | bytes 32800 | tf_op jit(solution)/shard_map/all_to_all | solution.py:11
  72.6 0.6 broadcast_in_dim.22
  73.2 4.0 %all-to-all-start.4 = ((f32[8,1,1024]{2,1,0:T(1,128)}), f32[8,1,1024]{2,1,0:T(1,128)S(1)}, u32[]{:S(2)}, u32[]{:S(2)}) async-start(f32[8,1,1024]{2,1,0:T(1,128)} %broadcast_in_dim.22), calls=%async_computation.4 | async-start | bytes 65536 | tf_op jit(solution)/shard_map/all_to_all | solution.py:11
  77.2 4.7 %all-to-all-done.4 = f32[8,1,1024]{2,1,0:T(1,128)S(1)} async-done(((f32[8,1,1024]{2,1,0:T(1,128)}), f32[8,1,1024]{2,1,0:T(1,128)S(1)}, u32[]{:S(2)}, u32[]{:S(2)}) %all-to-all-start.4) | async-done | bytes 32800 | tf_op jit(solution)/shard_map/all_to_all | solution.py:11
  81.9 0.6 broadcast_in_dim.21
  82.6 4.0 %all-to-all-start.3 = ((f32[8,1,1024]{2,1,0:T(1,128)}), f32[8,1,1024]{2,1,0:T(1,128)S(1)}, u32[]{:S(2)}, u32[]{:S(2)}) async-start(f32[8,1,1024]{2,1,0:T(1,128)} %broadcast_in_dim.21), calls=%async_computation.3 | async-start | bytes 65536 | tf_op jit(solution)/shard_map/all_to_all | solution.py:11
  86.6 4.7 %all-to-all-done.3 = f32[8,1,1024]{2,1,0:T(1,128)S(1)} async-done(((f32[8,1,1024]{2,1,0:T(1,128)}), f32[8,1,1024]{2,1,0:T(1,128)S(1)}, u32[]{:S(2)}, u32[]{:S(2)}) %all-to-all-start.3) | async-done | bytes 32800 | tf_op jit(solution)/shard_map/all_to_all | solution.py:11
  91.3 0.6 broadcast_in_dim.23
  91.9 4.0 %all-to-all-start.5 = ((f32[8,1,1024]{2,1,0:T(1,128)}), f32[8,1,1024]{2,1,0:T(1,128)S(1)}, u32[]{:S(2)}, u32[]{:S(2)}) async-start(f32[8,1,1024]{2,1,0:T(1,128)} %broadcast_in_dim.23), calls=%async_computation.5 | async-start | bytes 65536 | tf_op jit(solution)/shard_map/all_to_all | solution.py:11
  96.1 4.5 %all-to-all-done.5 = f32[8,1,1024]{2,1,0:T(1,128)S(1)} async-done(((f32[8,1,1024]{2,1,0:T(1,128)}), f32[8,1,1024]{2,1,0:T(1,128)S(1)}, u32[]{:S(2)}, u32[]{:S(2)}) %all-to-all-start.5) | async-done | bytes 32800 | tf_op jit(solution)/shard_map/all_to_all | solution.py:11
  100.7 1.3 %fusion.10 = (bf16[1,1,1792,128]{2,3,1,0:T(8,128)(2,1)S(1)}, bf16[1,1,1792,128]{2,3,1,0:T(8,128)(2,1)S(1)}) fusion(f32[1792,128]{0,1:T(8,128)S(1)} %get-tuple-element.53, f32[128]{0:T(128)S(1)} %get-tuple-element.39, f32[1792,128]{0,1:T(8,128)} %get-tuple-element.49, f32[128]{0:T(128)S(1)} %get-tuple-element.38), kind=kLoop, calls=%fused_computation.36 | loop fusion | flops 917504 | bytes 2753536 | tf_op jit(solution)/shard_map/stack | solution.py:97
  102.2 0.2 pad_maximum_fusion.1
  102.5 2.3 %copy.98 = bf16[4,1,1792,128]{3,2,1,0:T(8,128)(2,1)} copy(bf16[4,1,1792,128]{2,3,1,0:T(8,128)(2,1)S(1)} %pad_maximum_fusion.1) | data formatting | bytes 3670016
  104.8 2.5 %fusion.6 = (bf16[1,1,2,512,448]{3,4,2,1,0:T(8,128)(2,1)S(1)}, bf16[1,1,2,512,448]{3,4,2,1,0:T(8,128)(2,1)S(1)}) fusion(f32[2,512,448]{1,2,0:T(8,128)} %get-tuple-element.55, f32[2,448]{1,0:T(2,128)S(1)} %get-tuple-element.31, f32[2,512,448]{1,2,0:T(8,128)} %get-tuple-element.51, f32[2,448]{1,0:T(2,128)S(1)} %get-tuple-element.30), kind=kLoop, calls=%fused_computation.24 | loop fusion | flops 1835008 | bytes 5512192 | tf_op jit(solution)/shard_map/stack | solution.py:97
  107.4 0.6 copy-done.2
  108.0 0.3 fusion.4
  108.3 2.1 %pad_maximum_fusion = bf16[4,1,2,512,448]{3,4,2,1,0:T(8,128)(2,1)} fusion(bf16[1,1,2,512,448]{3,4,2,1,0:T(8,128)(2,1)S(1)} %get-tuple-element.59, bf16[1,1,2,512,448]{3,4,2,1,0:T(8,128)(2,1)S(1)} %get-tuple-element.58, bf16[1,1,2,512,448]{3,4,2,1,0:T(8,128)(2,1)S(1)} %get-tuple-element.57, bf16[1,1,2,512,448]{3,4,2,1,0:T(8,128)(2,1)S(1)} %get-tuple-element.56), kind=kLoop, calls=%fused_computation | loop fusion | flops 5505024 | bytes 7340032 | tf_op jit(solution)/shard_map/stack | solution.py:97
  (66 shorter events, 2.9 us)
Async XLA Ops:
  0.6 14.9 %copy-start = (bf16[4,1,56,16]{2,3,1,0:T(8,128)(2,1)S(1)}, bf16[4,1,56,16]{2,3,1,0:T(8,128)(2,1)}, u32[]{:S(2)}) copy-start(bf16[4,1,56,16]{2,3,1,0:T(8,128)(2,1)} %param.13) | copy-start | bytes 21508
  0.6 14.7 %copy-start.6 = (bf16[4,1,2,2,448]{4,3,2,1,0:T(2,128)(2,1)S(1)}, bf16[4,1,2,2,448]{4,3,2,1,0:T(2,128)(2,1)}, u32[]{:S(2)}) copy-start(bf16[4,1,2,2,448]{4,3,2,1,0:T(2,128)(2,1)} %param.10) | copy-start | bytes 43012
  3.5 33.0 %all-to-all-start = ((bf16[32,2,1024]{2,1,0:T(2,128)(2,1)}), bf16[32,2,1024]{2,1,0:T(2,128)(2,1)S(1)}, u32[]{:S(2)}, u32[]{:S(2)}) async-start(bf16[32,2,1024]{2,1,0:T(2,128)(2,1)} %reshape.406), calls=%async_computation | async-start | bytes 262144 | tf_op jit(solution)/shard_map/all_to_all | solution.py:11
  15.6 1.6 %copy-start.7 = (bf16[4,1,2,128]{3,2,1,0:T(2,128)(2,1)S(1)}, bf16[4,1,2,128]{3,2,1,0:T(2,128)(2,1)}, u32[]{:S(2)}) copy-start(bf16[4,1,2,128]{3,2,1,0:T(2,128)(2,1)} %param.14) | copy-start | bytes 6148
  36.6 24.1 %all-to-all-start.1 = ((bf16[32,2,1792]{2,1,0:T(2,128)(2,1)}), bf16[32,2,1792]{2,1,0:T(2,128)(2,1)S(1)}, u32[]{:S(2)}, u32[]{:S(2)}) async-start(bf16[32,2,1792]{2,1,0:T(2,128)(2,1)} %reshape.408), calls=%async_computation.1 | async-start | bytes 458752 | tf_op jit(solution)/shard_map/all_to_all | solution.py:11
  61.6 1.1 copy-start.4
  61.7 6.2 %copy-start.3 = (bf16[1,1,1792,128]{2,3,1,0:T(8,128)(2,1)S(1)}, bf16[1,1,1792,128]{2,3,1,0:T(8,128)(2,1)}, u32[]{:S(2)}) copy-start(bf16[1,1,1792,128]{2,3,1,0:T(8,128)(2,1)} %copy.109) | copy-start | bytes 1376260
  63.7 8.9 %all-to-all-start.2 = ((f32[8,1,1024]{2,1,0:T(1,128)}), f32[8,1,1024]{2,1,0:T(1,128)S(1)}, u32[]{:S(2)}, u32[]{:S(2)}) async-start(f32[8,1,1024]{2,1,0:T(1,128)} %broadcast_in_dim.20), calls=%async_computation.2 | async-start | bytes 65536 | tf_op jit(solution)/shard_map/all_to_all | solution.py:11
  68.3 32.3 %copy-start.8 = (f32[4,1,128]{2,1,0:T(1,128)S(1)}, f32[4,1,128]{2,1,0:T(1,128)}, u32[]{:S(2)}) copy-start(f32[4,1,128]{2,1,0:T(1,128)} %param.15) | copy-start | bytes 6148
  73.2 8.7 %all-to-all-start.4 = ((f32[8,1,1024]{2,1,0:T(1,128)}), f32[8,1,1024]{2,1,0:T(1,128)S(1)}, u32[]{:S(2)}, u32[]{:S(2)}) async-start(f32[8,1,1024]{2,1,0:T(1,128)} %broadcast_in_dim.22), calls=%async_computation.4 | async-start | bytes 65536 | tf_op jit(solution)/shard_map/all_to_all | solution.py:11
  82.6 8.7 %all-to-all-start.3 = ((f32[8,1,1024]{2,1,0:T(1,128)}), f32[8,1,1024]{2,1,0:T(1,128)S(1)}, u32[]{:S(2)}, u32[]{:S(2)}) async-start(f32[8,1,1024]{2,1,0:T(1,128)} %broadcast_in_dim.21), calls=%async_computation.3 | async-start | bytes 65536 | tf_op jit(solution)/shard_map/all_to_all | solution.py:11
  91.9 8.7 %all-to-all-start.5 = ((f32[8,1,1024]{2,1,0:T(1,128)}), f32[8,1,1024]{2,1,0:T(1,128)S(1)}, u32[]{:S(2)}, u32[]{:S(2)}) async-start(f32[8,1,1024]{2,1,0:T(1,128)} %broadcast_in_dim.23), calls=%async_computation.5 | async-start | bytes 65536 | tf_op jit(solution)/shard_map/all_to_all | solution.py:11
  102.5 2.3 %copy-start.5 = (f32[4,1,2,448]{3,2,1,0:T(2,128)S(1)}, f32[4,1,2,448]{3,2,1,0:T(2,128)}, u32[]{:S(2)}) copy-start(f32[4,1,2,448]{3,2,1,0:T(2,128)} %param.11) | copy-start | bytes 43012
  104.8 2.6 %copy-start.1 = (f32[2,512,448]{1,2,0:T(8,128)S(1)}, f32[2,512,448]{1,2,0:T(8,128)}, u32[]{:S(2)}) copy-start(f32[2,512,448]{1,2,0:T(8,128)} %get-tuple-element.47) | copy-start | bytes 5505028
  104.8 3.1 %copy-start.2 = (f32[2,512,448]{1,2,0:T(8,128)S(1)}, f32[2,512,448]{1,2,0:T(8,128)}, u32[]{:S(2)}) copy-start(f32[2,512,448]{1,2,0:T(8,128)} %get-tuple-element.43) | copy-start | bytes 5505028
where the time goes:
time: 111 us; the launch traced here: 110 us
  starting transfers between devices  37.4 us (34%)
  local copies, waits for them, and re-layouts  20.5 us (18%)
  waiting for transfers between devices  15.5 us (14%)
  matrix products  14.9 us (13%)
  blocking collectives  14.1 us (13%)
  other arithmetic  6.87 us (6%)
    all_to_all x6, starting transfers between devices, from_everyone(): lax.all_to_all(jnp.broadcast_to(value[None], (size, *value.shape)), axis,...  37.4 us
    all_to_all x6, waiting for transfers between devices, from_everyone(): lax.all_to_all(jnp.broadcast_to(value[None], (size, *value.shape)), axis,...  15.5 us
    dot_general x8, matrix products, combine_tile(): jnp.einsum('...ik,...kj->...ij', left, right, preferred_element_type=jnp....  14.9 us
    all_gather x1, blocking collectives, turned_gather(): lax.all_gather(both, axis, axis=0, tiled=True)  14.1 us
    unnamed x30, local copies, waits for them, and re-layouts  11.6 us
    another operation x6, other arithmetic, shards(): return (jnp.stack(inner_outputs), jnp.stack(outer_outputs))  6.63 us
    broadcast_in_dim x5, local copies, waits for them, and re-layouts, from_everyone(): jnp.broadcast_to(value[None], (size, *value.shape))  3.33 us
  transfers between devices with their start and end apart: 6, of which 4 were waited for; matrix products, arithmetic and copies ran while one was open for 23% of the time, Pallas kernels for 0%

commit v1 on v0

--- a/solution.py
+++ b/solution.py
@@ -4,6 +4,13 @@
 from jax.sharding import PartitionSpec as P
 
 epsilon = 1e-06
+
+
+def all_by_exchange(value, mesh_axis, dim):
+    size = lax.axis_size(mesh_axis)
+    shards = jnp.stack([value for _ in range(size)])
+    shards = lax.all_to_all(shards, mesh_axis, split_axis=0, concat_axis=0)
+    return jnp.concatenate(shards, axis=dim)
 
 
 def from_everyone(value, axis):
@@ -40,7 +47,7 @@
 def turned_gather(arrays, axis, dims):
     turned = [jnp.moveaxis(a, dim, 0) for a, dim in zip(arrays, dims)]
     both = jnp.concatenate([t.reshape(len(t), -1) for t in turned], axis=1)
-    result, at, finished = (lax.all_gather(both, axis, axis=0, tiled=True), 0, [])
+    result, at, finished = (all_by_exchange(both, axis, 0), 0, [])
     for t, dim in zip(turned, dims):
         section = result[:, at : at + t[0].size].reshape(-1, *t.shape[1:])
         finished.append(jnp.moveaxis(section, 0, dim))

time: 111 us -> 106 us (0.955)
  blocking collectives: 14.1 us -> 0 us
  waiting for transfers between devices: 15.5 us -> 20.1 us
  starting transfers between devices: 37.4 us -> 39.2 us
  local copies, waits for them, and re-layouts: 20.5 us -> 21.9 us
    all_gather x1 -> x0, blocking collectives: 14.1 us -> none  [turned_gather(): lax.all_gather(both, axis, axis=0, tiled=True)]
    all_to_all x0 -> x1, starting transfers between devices: none -> 6.47 us  [all_by_exchange(): shards = lax.all_to_all(shards, mesh_axis, split_axis=0, concat_axis=0)]
    all_to_all x6, starting transfers between devices: 37.4 us -> 32.8 us  [from_everyone(): lax.all_to_all(jnp.broadcast_to(value[None], (size, *value.shape)), axis,...]
    all_to_all x6, waiting for transfers between devices: 15.5 us -> 19.3 us  [from_everyone(): lax.all_to_all(jnp.broadcast_to(value[None], (size, *value.shape)), axis,...]
    another operation x8 -> x9, local copies, waits for them, and re-layouts: 2.03 us -> 2.76 us
    unnamed x30 -> x25, local copies, waits for them, and re-layouts: 11.6 us -> 11.5 us
  transfers between devices with their start and end apart: 6 -> 7, of which waited for: 4 -> 6; matrix products, arithmetic and copies ran while one was open for 23% -> 26% of each run, Pallas kernels for 0% -> 0%
where the time goes in v1:
time: 106 us; the launch traced here: 105 us
  starting transfers between devices  39.2 us (37%)
  local copies, waits for them, and re-layouts  21.9 us (21%)
  waiting for transfers between devices  20.1 us (19%)
  matrix products  15 us (14%)
  other arithmetic  7.6 us (7%)
    all_to_all x6, starting transfers between devices, from_everyone(): lax.all_to_all(jnp.broadcast_to(value[None], (size, *value.shape)), axis,...  32.8 us
    all_to_all x6, waiting for transfers between devices, from_everyone(): lax.all_to_all(jnp.broadcast_to(value[None], (size, *value.shape)), axis,...  19.3 us
    dot_general x8, matrix products, combine_tile(): jnp.einsum('...ik,...kj->...ij', left, right, preferred_element_type=jnp....  15 us
    unnamed x25, local copies, waits for them, and re-layouts  11.5 us
    another operation x6, other arithmetic, shards(): return (jnp.stack(inner_outputs), jnp.stack(outer_outputs))  6.68 us
    all_to_all x1, starting transfers between devices, all_by_exchange(): shards = lax.all_to_all(shards, mesh_axis, split_axis=0, concat_axis=0)  6.47 us
    broadcast_in_dim x5, local copies, waits for them, and re-layouts, from_everyone(): jnp.broadcast_to(value[None], (size, *value.shape))  3.32 us
  transfers between devices with their start and end apart: 7, of which 6 were waited for; matrix products, arithmetic and copies ran while one was open for 26% of the time, Pallas kernels for 0%

profile of v1, /device:TPU:1, one launch (start us, length us, event | category | flops | bytes accessed | tf_op | source)
XLA Modules:
  0.0 104.9 jit_solution(18319783553670352044)
XLA Ops:
  0.6 0.7 copy.79
  1.5 0.7 pad_maximum_fusion.2
  2.2 0.7 stack.41
  2.9 6.5 %all-to-all-start = ((bf16[8,2,4096]{2,1,0:T(2,128)(2,1)}), bf16[8,2,4096]{2,1,0:T(2,128)(2,1)S(1)}, u32[]{:S(2)}, u32[]{:S(2)}) async-start(bf16[8,2,4096]{2,1,0:T(2,128)(2,1)} %stack.41), calls=%async_computation | async-start | bytes 262144 | tf_op jit(solution)/shard_map/all_to_all | solution.py:12
  9.4 0.8 copy.81
  10.2 1.6 %fusion.20 = (bf16[1,1,1792,128]{3,2,1,0:T(8,128)(2,1)S(1)}, bf16[1,1,1792,128]{3,2,1,0:T(8,128)(2,1)S(1)}, bf16[1,1,1792,128]{3,2,1,0:T(8,128)(2,1)S(1)}, bf16[1,1,1792,128]{3,2,1,0:T(8,128)(2,1)S(1)}) fusion(bf16[4,1,1792,128]{3,2,1,0:T(8,128)(2,1)} %param.12), kind=kLoop, calls=%fused_computation.68 | loop fusion | bytes 3670016 | tf_op jit(solution)/shard_map/slice | solution.py:94
  12.0 1.8 %reshape.410 = bf16[32,2,1024]{2,1,0:T(2,128)(2,1)} reshape(bf16[32,4,1,2,16,16]{5,4,3,2,1,0:T(8,128)(2,1)S(1)} %broadcast_bitcast_fusion) | data formatting | bytes 262144
  13.8 0.8 all-to-all-done
  14.7 10.5 %all-to-all-start.1 = ((bf16[32,2,1024]{2,1,0:T(2,128)(2,1)}), bf16[32,2,1024]{2,1,0:T(2,128)(2,1)S(1)}, u32[]{:S(2)}, u32[]{:S(2)}) async-start(bf16[32,2,1024]{2,1,0:T(2,128)(2,1)} %reshape.410), calls=%async_computation.1 | async-start | bytes 262144 | tf_op jit(solution)/shard_map/all_to_all | solution.py:18
  25.3 1.7 %reshape.412 = bf16[32,2,1792]{2,1,0:T(2,128)(2,1)} reshape(bf16[32,4,1,16,56]{4,3,2,1,0:T(8,128)(2,1)S(1)} %broadcast_bitcast_fusion.1) | data formatting | bytes 458752
  26.9 1.0 copy.107
  27.9 1.0 copy.109
  28.9 1.0 copy.108
  30.5 3.8 %all-to-all-done.1 = bf16[32,2,1024]{2,1,0:T(2,128)(2,1)S(1)} async-done(((bf16[32,2,1024]{2,1,0:T(2,128)(2,1)}), bf16[32,2,1024]{2,1,0:T(2,128)(2,1)S(1)}, u32[]{:S(2)}, u32[]{:S(2)}) %all-to-all-start.1) | async-done | bytes 131104 | tf_op jit(solution)/shard_map/all_to_all | solution.py:18
  34.3 5.4 %all-to-all-start.2 = ((bf16[32,2,1792]{2,1,0:T(2,128)(2,1)}), bf16[32,2,1792]{2,1,0:T(2,128)(2,1)S(1)}, u32[]{:S(2)}, u32[]{:S(2)}) async-start(bf16[32,2,1792]{2,1,0:T(2,128)(2,1)} %reshape.412), calls=%async_computation.2 | async-start | bytes 458752 | tf_op jit(solution)/shard_map/all_to_all | solution.py:18
  39.8 0.7 reshape.411
  40.9 0.3 reshape.382
  41.4 0.3 reshape.398
  41.8 0.3 reshape.393
  42.2 0.3 reshape.388
  42.5 2.9 %multiply_reduce_fusion.2 = (f32[2,448]{1,0:T(2,128)S(1)}, f32[2,512,448]{1,2,0:T(8,128)}) fusion(bf16[2,512,16]{1,2,0:T(8,128)(2,1)S(1)} %reshape.388, bf16[4,1,2,16,448]{4,3,2,1,0:T(8,128)(2,1)S(1)} %bitcast.185, bf16[4,1,2,512,448]{3,4,2,1,0:T(8,128)(2,1)} %param.8), kind=kOutput, calls=%fused_computation.19 | convolution fusion | flops 16514176 | bytes 2821632 | tf_op jit(solution)/shard_map/...ik,...kj->...ij/dot_general | solution.py:59
  45.5 2.9 %multiply_reduce_fusion.1 = (f32[2,448]{1,0:T(2,128)S(1)}, f32[2,512,448]{1,2,0:T(8,128)}) fusion(bf16[2,512,16]{1,2,0:T(8,128)(2,1)S(1)} %reshape.393, bf16[4,1,2,16,448]{4,3,2,1,0:T(8,128)(2,1)S(1)} %bitcast.186, bf16[4,1,2,512,448]{3,4,2,1,0:T(8,128)(2,1)} %param.8), kind=kOutput, calls=%fused_computation.17 | convolution fusion | flops 16514176 | bytes 2821632 | tf_op jit(solution)/shard_map/...ik,...kj->...ij/dot_general | solution.py:59
  48.4 2.9 %multiply_reduce_fusion = (f32[2,448]{1,0:T(2,128)S(1)}, f32[2,512,448]{1,2,0:T(8,128)}) fusion(bf16[2,512,16]{1,2,0:T(8,128)(2,1)S(1)} %reshape.398, bf16[4,1,2,16,448]{4,3,2,1,0:T(8,128)(2,1)S(1)} %bitcast.187, bf16[4,1,2,512,448]{3,4,2,1,0:T(8,128)(2,1)} %param.8), kind=kOutput, calls=%fused_computation.15 | convolution fusion | flops 16514176 | bytes 2821632 | tf_op jit(solution)/shard_map/...ik,...kj->...ij/dot_general | solution.py:59
  51.4 2.9 %multiply_reduce_fusion.3 = (f32[2,448]{1,0:T(2,128)S(1)}, f32[2,512,448]{1,2,0:T(8,128)}) fusion(bf16[2,512,16]{1,2,0:T(8,128)(2,1)S(1)} %reshape.382, bf16[4,1,2,16,448]{4,3,2,1,0:T(8,128)(2,1)S(1)} %bitcast.188, bf16[4,1,2,512,448]{3,4,2,1,0:T(8,128)(2,1)} %param.8), kind=kOutput, calls=%fused_computation.21 | convolution fusion | flops 16514176 | bytes 2821632 | tf_op jit(solution)/shard_map/...ik,...kj->...ij/dot_general | solution.py:59
  54.4 0.9 reshape.413
  56.3 0.4 multiply_reduce_fusion.7
  56.7 0.6 broadcast_in_dim.20
  57.4 4.9 %all-to-all-start.3 = ((f32[8,1,1024]{2,1,0:T(1,128)}), f32[8,1,1024]{2,1,0:T(1,128)S(1)}, u32[]{:S(2)}, u32[]{:S(2)}) async-start(f32[8,1,1024]{2,1,0:T(1,128)} %broadcast_in_dim.20), calls=%async_computation.3 | async-start | bytes 65536 | tf_op jit(solution)/shard_map/all_to_all | solution.py:18
  62.3 0.4 multiply_reduce_fusion.5
  62.7 1.4 %multiply_reduce_fusion.6 = (f32[128]{0:T(128)S(1)}, f32[1792,128]{0,1:T(8,128)S(1)}) fusion(bf16[1792,16]{0,1:T(8,128)(2,1)S(1)} %reshape.391, bf16[1,1,16,128]{3,0,2,1:T(2,128)(2,1)S(1)} %get-tuple-element.35, bf16[1,1,1792,128]{2,3,1,0:T(8,128)(2,1)} %copy.108), kind=kOutput, calls=%fused_computation.32 | convolution fusion | flops 8257408 | bytes 1438208 | tf_op jit(solution)/shard_map/...ik,...kj->...ij/dot_general | solution.py:59
  64.2 1.2 %multiply_reduce_fusion.4 = (f32[128]{0:T(128)S(1)}, f32[1792,128]{0,1:T(8,128)}) fusion(bf16[1792,16]{0,1:T(8,128)(2,1)S(1)} %reshape.401, bf16[1,1,16,128]{3,0,2,1:T(2,128)(2,1)S(1)} %get-tuple-element.33, bf16[1,1,1792,128]{2,3,1,0:T(8,128)(2,1)S(1)} %copy.110), kind=kOutput, calls=%fused_computation.30 | convolution fusion | flops 8257408 | bytes 1438208 | tf_op jit(solution)/shard_map/...ik,...kj->...ij/dot_general | solution.py:59
  65.4 1.6 %all-to-all-done.3 = f32[8,1,1024]{2,1,0:T(1,128)S(1)} async-done(((f32[8,1,1024]{2,1,0:T(1,128)}), f32[8,1,1024]{2,1,0:T(1,128)S(1)}, u32[]{:S(2)}, u32[]{:S(2)}) %all-to-all-start.3) | async-done | bytes 32800 | tf_op jit(solution)/shard_map/all_to_all | solution.py:18
  67.1 0.6 broadcast_in_dim.22
  67.7 4.0 %all-to-all-start.5 = ((f32[8,1,1024]{2,1,0:T(1,128)}), f32[8,1,1024]{2,1,0:T(1,128)S(1)}, u32[]{:S(2)}, u32[]{:S(2)}) async-start(f32[8,1,1024]{2,1,0:T(1,128)} %broadcast_in_dim.22), calls=%async_computation.5 | async-start | bytes 65536 | tf_op jit(solution)/shard_map/all_to_all | solution.py:18
  71.7 4.7 %all-to-all-done.5 = f32[8,1,1024]{2,1,0:T(1,128)S(1)} async-done(((f32[8,1,1024]{2,1,0:T(1,128)}), f32[8,1,1024]{2,1,0:T(1,128)S(1)}, u32[]{:S(2)}, u32[]{:S(2)}) %all-to-all-start.5) | async-done | bytes 32800 | tf_op jit(solution)/shard_map/all_to_all | solution.py:18
  76.4 0.6 broadcast_in_dim.21
  77.0 4.0 %all-to-all-start.4 = ((f32[8,1,1024]{2,1,0:T(1,128)}), f32[8,1,1024]{2,1,0:T(1,128)S(1)}, u32[]{:S(2)}, u32[]{:S(2)}) async-start(f32[8,1,1024]{2,1,0:T(1,128)} %broadcast_in_dim.21), calls=%async_computation.4 | async-start | bytes 65536 | tf_op jit(solution)/shard_map/all_to_all | solution.py:18
  81.0 4.7 %all-to-all-done.4 = f32[8,1,1024]{2,1,0:T(1,128)S(1)} async-done(((f32[8,1,1024]{2,1,0:T(1,128)}), f32[8,1,1024]{2,1,0:T(1,128)S(1)}, u32[]{:S(2)}, u32[]{:S(2)}) %all-to-all-start.4) | async-done | bytes 32800 | tf_op jit(solution)/shard_map/all_to_all | solution.py:18
  85.7 0.6 broadcast_in_dim.23
  86.3 4.0 %all-to-all-start.6 = ((f32[8,1,1024]{2,1,0:T(1,128)}), f32[8,1,1024]{2,1,0:T(1,128)S(1)}, u32[]{:S(2)}, u32[]{:S(2)}) async-start(f32[8,1,1024]{2,1,0:T(1,128)} %broadcast_in_dim.23), calls=%async_computation.6 | async-start | bytes 65536 | tf_op jit(solution)/shard_map/all_to_all | solution.py:18
  90.5 4.5 %all-to-all-done.6 = f32[8,1,1024]{2,1,0:T(1,128)S(1)} async-done(((f32[8,1,1024]{2,1,0:T(1,128)}), f32[8,1,1024]{2,1,0:T(1,128)S(1)}, u32[]{:S(2)}, u32[]{:S(2)}) %all-to-all-start.6) | async-done | bytes 32800 | tf_op jit(solution)/shard_map/all_to_all | solution.py:18
  95.2 1.3 %fusion.10 = (bf16[1,1,1792,128]{2,3,1,0:T(8,128)(2,1)S(1)}, bf16[1,1,1792,128]{2,3,1,0:T(8,128)(2,1)S(1)}) fusion(f32[1792,128]{0,1:T(8,128)S(1)} %get-tuple-element.53, f32[128]{0:T(128)S(1)} %get-tuple-element.39, f32[1792,128]{0,1:T(8,128)} %get-tuple-element.49, f32[128]{0:T(128)S(1)} %get-tuple-element.38), kind=kLoop, calls=%fused_computation.36 | loop fusion | flops 917504 | bytes 2753536 | tf_op jit(solution)/shard_map/stack | solution.py:104
  96.7 0.2 pad_maximum_fusion.1
  96.9 2.3 %copy.98 = bf16[4,1,1792,128]{3,2,1,0:T(8,128)(2,1)} copy(bf16[4,1,1792,128]{2,3,1,0:T(8,128)(2,1)S(1)} %pad_maximum_fusion.1) | data formatting | bytes 3670016
  99.3 2.5 %fusion.6 = (bf16[1,1,2,512,448]{3,4,2,1,0:T(8,128)(2,1)S(1)}, bf16[1,1,2,512,448]{3,4,2,1,0:T(8,128)(2,1)S(1)}) fusion(f32[2,512,448]{1,2,0:T(8,128)} %get-tuple-element.55, f32[2,448]{1,0:T(2,128)S(1)} %get-tuple-element.31, f32[2,512,448]{1,2,0:T(8,128)} %get-tuple-element.51, f32[2,448]{1,0:T(2,128)S(1)} %get-tuple-element.30), kind=kLoop, calls=%fused_computation.24 | loop fusion | flops 1835008 | bytes 5512192 | tf_op jit(solution)/shard_map/stack | solution.py:104
  101.9 0.6 copy-done.2
  102.4 0.4 fusion.4
  102.8 2.1 %pad_maximum_fusion = bf16[4,1,2,512,448]{3,4,2,1,0:T(8,128)(2,1)} fusion(bf16[1,1,2,512,448]{3,4,2,1,0:T(8,128)(2,1)S(1)} %get-tuple-element.59, bf16[1,1,2,512,448]{3,4,2,1,0:T(8,128)(2,1)S(1)} %get-tuple-element.58, bf16[1,1,2,512,448]{3,4,2,1,0:T(8,128)(2,1)S(1)} %get-tuple-element.57, bf16[1,1,2,512,448]{3,4,2,1,0:T(8,128)(2,1)S(1)} %get-tuple-element.56), kind=kLoop, calls=%fused_computation | loop fusion | flops 5505024 | bytes 7340032 | tf_op jit(solution)/shard_map/stack | solution.py:104
  (64 shorter events, 3.9 us)
Async XLA Ops:
  0.6 24.5 %copy-start = (bf16[4,1,56,16]{2,3,1,0:T(8,128)(2,1)S(1)}, bf16[4,1,56,16]{2,3,1,0:T(8,128)(2,1)}, u32[]{:S(2)}) copy-start(bf16[4,1,56,16]{2,3,1,0:T(8,128)(2,1)} %param.13) | copy-start | bytes 21508
  2.9 11.7 %all-to-all-start = ((bf16[8,2,4096]{2,1,0:T(2,128)(2,1)}), bf16[8,2,4096]{2,1,0:T(2,128)(2,1)S(1)}, u32[]{:S(2)}, u32[]{:S(2)}) async-start(bf16[8,2,4096]{2,1,0:T(2,128)(2,1)} %stack.41), calls=%async_computation | async-start | bytes 262144 | tf_op jit(solution)/shard_map/all_to_all | solution.py:12
  14.7 19.7 %all-to-all-start.1 = ((bf16[32,2,1024]{2,1,0:T(2,128)(2,1)}), bf16[32,2,1024]{2,1,0:T(2,128)(2,1)S(1)}, u32[]{:S(2)}, u32[]{:S(2)}) async-start(bf16[32,2,1024]{2,1,0:T(2,128)(2,1)} %reshape.410), calls=%async_computation.1 | async-start | bytes 262144 | tf_op jit(solution)/shard_map/all_to_all | solution.py:18
  34.3 20.1 %all-to-all-start.2 = ((bf16[32,2,1792]{2,1,0:T(2,128)(2,1)}), bf16[32,2,1792]{2,1,0:T(2,128)(2,1)S(1)}, u32[]{:S(2)}, u32[]{:S(2)}) async-start(bf16[32,2,1792]{2,1,0:T(2,128)(2,1)} %reshape.412), calls=%async_computation.2 | async-start | bytes 458752 | tf_op jit(solution)/shard_map/all_to_all | solution.py:18
  55.3 1.1 %copy-start.4 = (bf16[1,1,1792,128]{2,3,1,0:T(8,128)(2,1)S(1)}, bf16[1,1,1792,128]{2,3,1,0:T(8,128)(2,1)}, u32[]{:S(2)}) copy-start(bf16[1,1,1792,128]{2,3,1,0:T(8,128)(2,1)} %copy.107) | copy-start | bytes 1376260
  55.4 7.0 %copy-start.3 = (bf16[1,1,1792,128]{2,3,1,0:T(8,128)(2,1)S(1)}, bf16[1,1,1792,128]{2,3,1,0:T(8,128)(2,1)}, u32[]{:S(2)}) copy-start(bf16[1,1,1792,128]{2,3,1,0:T(8,128)(2,1)} %copy.109) | copy-start | bytes 1376260
  57.4 9.7 %all-to-all-start.3 = ((f32[8,1,1024]{2,1,0:T(1,128)}), f32[8,1,1024]{2,1,0:T(1,128)S(1)}, u32[]{:S(2)}, u32[]{:S(2)}) async-start(f32[8,1,1024]{2,1,0:T(1,128)} %broadcast_in_dim.20), calls=%async_computation.3 | async-start | bytes 65536 | tf_op jit(solution)/shard_map/all_to_all | solution.py:18
  62.7 32.3 %copy-start.6 = (f32[4,1,128]{2,1,0:T(1,128)S(1)}, f32[4,1,128]{2,1,0:T(1,128)}, u32[]{:S(2)}) copy-start(f32[4,1,128]{2,1,0:T(1,128)} %param.15) | copy-start | bytes 6148
  67.7 8.7 %all-to-all-start.5 = ((f32[8,1,1024]{2,1,0:T(1,128)}), f32[8,1,1024]{2,1,0:T(1,128)S(1)}, u32[]{:S(2)}, u32[]{:S(2)}) async-start(f32[8,1,1024]{2,1,0:T(1,128)} %broadcast_in_dim.22), calls=%async_computation.5 | async-start | bytes 65536 | tf_op jit(solution)/shard_map/all_to_all | solution.py:18
  77.0 8.7 %all-to-all-start.4 = ((f32[8,1,1024]{2,1,0:T(1,128)}), f32[8,1,1024]{2,1,0:T(1,128)S(1)}, u32[]{:S(2)}, u32[]{:S(2)}) async-start(f32[8,1,1024]{2,1,0:T(1,128)} %broadcast_in_dim.21), calls=%async_computation.4 | async-start | bytes 65536 | tf_op jit(solution)/shard_map/all_to_all | solution.py:18
  86.3 8.7 %all-to-all-start.6 = ((f32[8,1,1024]{2,1,0:T(1,128)}), f32[8,1,1024]{2,1,0:T(1,128)S(1)}, u32[]{:S(2)}, u32[]{:S(2)}) async-start(f32[8,1,1024]{2,1,0:T(1,128)} %broadcast_in_dim.23), calls=%async_computation.6 | async-start | bytes 65536 | tf_op jit(solution)/shard_map/all_to_all | solution.py:18
  96.9 2.3 %copy-start.5 = (f32[4,1,2,448]{3,2,1,0:T(2,128)S(1)}, f32[4,1,2,448]{3,2,1,0:T(2,128)}, u32[]{:S(2)}) copy-start(f32[4,1,2,448]{3,2,1,0:T(2,128)} %param.11) | copy-start | bytes 43012
  99.3 2.6 %copy-start.1 = (f32[2,512,448]{1,2,0:T(8,128)S(1)}, f32[2,512,448]{1,2,0:T(8,128)}, u32[]{:S(2)}) copy-start(f32[2,512,448]{1,2,0:T(8,128)} %get-tuple-element.47) | copy-start | bytes 5505028
  99.3 3.1 %copy-start.2 = (f32[2,512,448]{1,2,0:T(8,128)S(1)}, f32[2,512,448]{1,2,0:T(8,128)}, u32[]{:S(2)}) copy-start(f32[2,512,448]{1,2,0:T(8,128)} %get-tuple-element.43) | copy-start | bytes 5505028
